TPU v7x, 32 devices: a whole 2x2x4 slice. The times are simulated.
32 devices in a mesh: samp: 16 (over z, y, x), feat: 2 (over core).
Axes of the slice: x: 2, y: 2, z: 4, core: 2. Of those that a mesh axis runs over, the one named last changes fastest.
Arguments:
- design_matrix: bfloat16 [2048, 32768], P('samp', 'feat'), may hold values from -0.046875 to 0.046875
- labels: int32 [2048], P('samp'), may hold values from 0 to 1
- weights: float32 [16, 32768], P(None, ('feat', 'samp')), may hold values from -6 to 6
- lambdas: float32 [16], replicated, may hold values from 0.05 to 1
- sketch: bfloat16 [32768, 384], P(('feat', 'samp')), may hold values from -0.03125 to 0.03125
- sketch_values: float32 [384], replicated, may hold values from 0.05 to 2
Outputs:
- new_weights: float32 [16, 32768], P(None, ('feat', 'samp'))
All inputs are finite; a program needn't handle non-finite values.
Results may differ from a plain program's by a relative error of at most 0.004.
Values may be sent and summed in bfloat16 or wider, within the bound.
No kernel may reach another device: no remote copies, remote signals or barrier semaphores. Data moves between devices by JAX's collectives and lax.ppermute only.
A program may use at most 64 MiB of HBM per device.

v0:
```python
import jax
import jax.numpy as jnp
from jax import lax
from jax.sharding import PartitionSpec as P

ITERS = 2


def shards(design_matrix, labels, weights, lambdas, sketch, sketch_values):
    sketch_full = sketch.astype(jnp.float32)
    smallest = jnp.min(sketch_values)
    ratios = (smallest + lambdas[:, None]) / (sketch_values[None, :] + lambdas[:, None]) - 1.0

    def apply_rows(vector):
        vector_half = vector.astype(jnp.bfloat16)
        partial_rows = lax.dot_general(
            lax.all_gather(vector_half, "samp", axis=1, tiled=True),
            design_matrix,
            (((1,), (1,)), ((), ())),
            preferred_element_type=jnp.float32,
        )
        return lax.psum(partial_rows, "feat")

    def apply_columns(values):
        return lax.psum_scatter(
            lax.dot_general(
                design_matrix, values, (((0,), (1,)), ((), ())), preferred_element_type=jnp.float32
            ),
            "samp",
            scatter_dimension=0,
            tiled=True,
        ).T

    def precondition(residual):
        projected = jnp.dot(residual, sketch_full, precision=lax.Precision.HIGHEST)
        projected = lax.psum(projected, ("samp", "feat"))
        correction = lax.dot_general(
            ratios * projected,
            sketch_full,
            (((1,), (1,)), ((), ())),
            precision=lax.Precision.HIGHEST,
        )
        precond_res = residual + correction
        res_dot = lax.psum(jnp.sum(residual * precond_res, axis=1), ("samp", "feat"))
        return (precond_res, res_dot)

    logits = apply_rows(weights)
    probability = jax.nn.sigmoid(logits)
    hessian_diag = probability * (1.0 - probability)
    miss_rows = (probability - labels[None, :].astype(jnp.float32)).astype(jnp.bfloat16)
    gradient = apply_columns(miss_rows) + lambdas[:, None] * weights
    residual = -gradient
    precond_res, res_dot = precondition(residual)
    direction = precond_res
    update = jnp.zeros_like(residual)
    for iteration in range(ITERS):
        image_rows = apply_rows(direction)
        hess_dir = (
            apply_columns((hessian_diag * image_rows).astype(jnp.bfloat16))
            + lambdas[:, None] * direction
        )
        curvature = lax.psum(jnp.sum(direction * hess_dir, axis=1), ("samp", "feat"))
        step_size = res_dot / curvature
        update = update + step_size[:, None] * direction
        if iteration + 1 < ITERS:
            residual = residual - step_size[:, None] * hess_dir
            precond_res, new_dot = precondition(residual)
            direction = precond_res + (new_dot / res_dot)[:, None] * direction
            res_dot = new_dot
    return weights + update


def solution(mesh):
    return jax.shard_map(
        shards,
        mesh=mesh,
        in_specs=(
            P("samp", "feat"),
            P("samp"),
            P(None, ("feat", "samp")),
            P(),
            P(("feat", "samp"), None),
            P(),
        ),
        out_specs=P(None, ("feat", "samp")),
        check_vma=False,
    )
```

profile of v0, /device:TPU:10, one launch (start us, length us, event | category | flops | bytes accessed | tf_op | source)
XLA Modules:
  0.0 596.1 jit_solution(18189731865618623638)
XLA Ops:
  6.5 0.0 copy-start
  6.5 0.0 reduce-scatter.4.cloned.1.call-start
  6.5 0.7 convert_element_type.24
  7.3 0.8 convert_element_type.23
  8.1 33.0 %all_gather.9 = bf16[16,16384]{1,0:T(8,128)(2,1)S(1)} all-gather(bf16[16,1024]{1,0:T(8,128)(2,1)S(1)} %convert_element_type.23), channel_id=1, replica_groups=mesh['samp'=16,'feat'=2] {'samp'}, dimensions={1}, use_global_device_ids=true | all-gather | bytes 557056 | tf_op jit(solution)/shard_map/all_gather | solution.py:17
  41.1 3.4 fusion.22
  44.4 0.0 copy-start.3
  44.4 0.0 copy-start.2
  44.4 0.0 copy-start.1
  44.5 2.6 psum.63
  47.1 3.8 convolution_bitcast_fusion.2
  51.0 0.0 reduce-scatter.4.cloned.1.call-update
  51.0 0.0 reduce-scatter.6.cloned.1.call-start
  51.0 0.0 copy-done.3
  51.0 0.6 reduce_min.9
  51.6 0.0 copy-done.2
  51.6 0.6 broadcast_add_fusion
  52.3 73.3 %reduce-scatter.4.cloned.1.call-done = f32[1024,16]{0,1:T(8,128)} async-done(((f32[16384,16]{0,1:T(8,128)}), f32[1024,16]{0,1:T(8,128)}) %reduce-scatter.4.cloned.1.call-update) | async-done | bytes 65552 | tf_op jit(solution)/shard_map/reduce_scatter | solution.py:25
  125.6 0.0 copy-done.1
  125.6 0.9 fusion.2
  126.6 0.0 copy-done
  126.6 0.4 fusion.23
  127.0 50.1 %psum.64 = f32[16,384]{1,0:T(8,128)S(1)} all-reduce(f32[16,384]{1,0:T(8,128)S(1)} %fusion.23), channel_id=1, replica_groups=mesh['samp'=16,'feat'=2] {'samp','feat'}, use_global_device_ids=true, to_apply=%region_3.0 | all-reduce | flops 6144 | bytes 49152 | tf_op jit(solution)/shard_map/psum | solution.py:36
  177.1 0.7 fusion.21
  177.8 32.0 %all_gather.10 = bf16[16,16384]{1,0:T(8,128)(2,1)S(1)} all-gather(bf16[16,1024]{1,0:T(8,128)(2,1)S(1)} %get-tuple-element.9), channel_id=1, replica_groups=mesh['samp'=16,'feat'=2] {'samp'}, dimensions={1}, use_global_device_ids=true | all-gather | bytes 557056 | tf_op jit(solution)/shard_map/all_gather | solution.py:17
  209.8 3.4 fusion.24
  213.1 2.5 psum.66
  215.6 3.8 convolution_bitcast_fusion.1
  219.5 0.0 reduce-scatter.6.cloned.1.call-update
  219.5 0.0 reduce-scatter.8.cloned.1.call-start
  219.5 71.6 %reduce-scatter.6.cloned.1.call-done = f32[1024,16]{0,1:T(8,128)} async-done(((f32[16384,16]{0,1:T(8,128)}), f32[1024,16]{0,1:T(8,128)}) %reduce-scatter.6.cloned.1.call-update) | async-done | bytes 65552 | tf_op jit(solution)/shard_map/reduce_scatter | solution.py:25
  291.1 1.0 multiply_reduce_fusion.1
  292.1 49.7 %all-reduce = (f32[16]{0:T(128)S(1)}, f32[16]{0:T(128)S(1)}) all-reduce(f32[16]{0:T(128)S(1)} %get-tuple-element.6, f32[16]{0:T(128)S(1)} %get-tuple-element.5), channel_id=1, replica_groups=mesh['samp'=16,'feat'=2] {'samp','feat'}, use_global_device_ids=true, to_apply=%region_5.0 | all-reduce | flops 32 | bytes 256 | tf_op jit(solution)/shard_map/psum | solution.py:44
  341.9 0.9 multiply_subtract_fusion
  342.8 0.4 fusion.25
  343.2 38.3 %psum.68 = f32[16,384]{1,0:T(8,128)S(1)} all-reduce(f32[16,384]{1,0:T(8,128)S(1)} %fusion.25), channel_id=1, replica_groups=mesh['samp'=16,'feat'=2] {'samp','feat'}, use_global_device_ids=true, to_apply=%region_10.0 | all-reduce | flops 6144 | bytes 49152 | tf_op jit(solution)/shard_map/psum | solution.py:36
  381.5 0.8 multiply_reduce_fusion
  382.3 41.9 %psum.69 = f32[16]{0:T(128)S(1)} all-reduce(f32[16]{0:T(128)S(1)} %get-tuple-element.11), channel_id=1, replica_groups=mesh['samp'=16,'feat'=2] {'samp','feat'}, use_global_device_ids=true, to_apply=%region_12.0 | all-reduce | flops 16 | bytes 128 | tf_op jit(solution)/shard_map/psum | solution.py:44
  424.2 0.1 fusion.20
  424.3 31.8 %all_gather.11 = bf16[16,16384]{1,0:T(8,128)(2,1)S(1)} all-gather(bf16[16,1024]{1,0:T(8,128)(2,1)S(1)} %fusion.20), channel_id=1, replica_groups=mesh['samp'=16,'feat'=2] {'samp'}, dimensions={1}, use_global_device_ids=true | all-gather | bytes 557056 | tf_op jit(solution)/shard_map/all_gather | solution.py:17
  456.1 3.4 fusion.26
  459.5 2.5 psum.70
  462.0 3.9 convolution_bitcast_fusion
  465.8 0.0 reduce-scatter.8.cloned.1.call-update
  465.8 72.2 %reduce-scatter.8.cloned.1.call-done = f32[1024,16]{0,1:T(8,128)} async-done(((f32[16384,16]{0,1:T(8,128)}), f32[1024,16]{0,1:T(8,128)}) %reduce-scatter.8.cloned.1.call-update) | async-done | bytes 65552 | tf_op jit(solution)/shard_map/reduce_scatter | solution.py:25
  538.1 1.0 fusion.1
  539.1 49.8 %psum.71 = f32[16]{0:T(128)S(1)} all-reduce(f32[16]{0:T(128)S(1)} %fusion.1), channel_id=1, replica_groups=mesh['samp'=16,'feat'=2] {'samp','feat'}, use_global_device_ids=true, to_apply=%region_16.0 | all-reduce | flops 16 | bytes 128 | tf_op jit(solution)/shard_map/psum | solution.py:62
  588.9 0.7 add_add_fusion
  (3 shorter events, 0.0 us)
Async XLA Ops:
  6.5 120.0 %copy-start = (bf16[1024,384]{1,0:T(8,128)(2,1)S(1)}, bf16[1024,384]{1,0:T(8,128)(2,1)}, u32[]{:S(2)}) copy-start(bf16[1024,384]{1,0:T(8,128)(2,1)} %param.10) | copy-start | bytes 2359300
  6.5 119.1 %reduce-scatter.4.cloned.1.call-start = ((), (), s32[]{:S(2)}) async-start(), calls=%async_computation.3 | async-start | bytes 1114112 | tf_op jit(solution)/shard_map/reduce_scatter | solution.py:25
  44.4 6.6 %copy-start.3 = (f32[384]{0:T(512)S(1)}, f32[384]{0:T(512)}, u32[]{:S(2)}) copy-start(f32[384]{0:T(512)} %param.11) | copy-start | bytes 4612
  44.4 7.2 %copy-start.2 = (f32[16]{0:T(128)S(1)}, f32[16]{0:T(128)}, u32[]{:S(2)}) copy-start(f32[16]{0:T(128)} %param.9) | copy-start | bytes 196
  44.4 81.2 %copy-start.1 = (f32[16,1024]{1,0:T(8,128)S(1)}, f32[16,1024]{1,0:T(8,128)}, u32[]{:S(2)}) copy-start(f32[16,1024]{1,0:T(8,128)} %param.8) | copy-start | bytes 196612
  51.0 240.1 %reduce-scatter.6.cloned.1.call-start = ((), (), s32[]{:S(2)}) async-start(), calls=%async_computation.4 | async-start | bytes 1114112 | tf_op jit(solution)/shard_map/reduce_scatter | solution.py:25
  219.5 318.6 %reduce-scatter.8.cloned.1.call-start = ((), (), s32[]{:S(2)}) async-start(), calls=%async_computation.5 | async-start | bytes 1114112 | tf_op jit(solution)/shard_map/reduce_scatter | solution.py:25
Sparse Core Ops, SparseCore 0:
  51.1 74.4 reduce-scatter.3
  219.6 71.4 reduce-scatter.5
  466.0 72.0 reduce-scatter.7
where the time goes:
time: 597 us; the launch traced here: 596 us
  blocking collectives  334 us (56%)
  waiting for transfers between devices  217 us (36%)
  matrix products  24.1 us (4%)
  between operations  13.2 us (2%)
  other arithmetic  7.54 us (1%)
    reduce_scatter x3, waiting for transfers between devices, apply_columns(): lax.psum_scatter(lax.dot_general(design_matrix, values, (((0,), (1,)), ((...  217 us
    all_gather x3, blocking collectives, apply_rows(): lax.all_gather(vector_half, 'samp', axis=1, tiled=True)  96.7 us
    psum x2, blocking collectives, precondition(): lax.psum(jnp.sum(residual * precond_res, axis=1), ('samp', 'feat'))  91.6 us
    psum x2, blocking collectives, precondition(): projected = lax.psum(projected, ('samp', 'feat'))  88.3 us
    psum x1, blocking collectives, shards(): lax.psum(jnp.sum(direction * hess_dir, axis=1), ('samp', 'feat'))  49.8 us
  transfers between devices with their start and end apart: 3, of which 3 were waited for; matrix products, arithmetic and copies ran while one was open for 0% of the time, Pallas kernels for 0%

commit v1 on v0

--- a/solution.py
+++ b/solution.py
@@ -32,6 +32,12 @@
         ).T
 
     def precondition(residual):
+
+        def work_lanes(xin):
+            for dev_j in ("samp", "feat"):
+                xin = jax.lax.psum(xin, dev_j)
+            return xin
+
         projected = jnp.dot(residual, sketch_full, precision=lax.Precision.HIGHEST)
         projected = lax.psum(projected, ("samp", "feat"))
         correction = lax.dot_general(
@@ -41,7 +47,7 @@
             precision=lax.Precision.HIGHEST,
         )
         precond_res = residual + correction
-        res_dot = lax.psum(jnp.sum(residual * precond_res, axis=1), ("samp", "feat"))
+        res_dot = work_lanes(jnp.sum(residual * precond_res, axis=1))
         return (precond_res, res_dot)
 
     logits = apply_rows(weights)

time: 597 us -> 637 us (1.067)
  blocking collectives: 334 us -> 375 us
    psum x1 -> x2, blocking collectives: 49.8 us -> 99.5 us  [shards(): lax.psum(jnp.sum(direction * hess_dir, axis=1), ('samp', 'feat'))]
    psum x2 -> x4, blocking collectives: 91.6 us -> 63.1 us  [work_lanes(): xin = jax.lax.psum(xin, dev_j)]
    psum x2, blocking collectives: 88.3 us -> 98 us  [precondition(): projected = lax.psum(projected, ('samp', 'feat'))]
    all_gather x3, blocking collectives: 96.7 us -> 106 us  [apply_rows(): lax.all_gather(vector_half, 'samp', axis=1, tiled=True)]
where the time goes in v1:
time: 637 us; the launch traced here: 636 us
  blocking collectives  375 us (59%)
  waiting for transfers between devices  217 us (34%)
  matrix products  24.1 us (4%)
  between operations  13.2 us (2%)
  other arithmetic  7.54 us (1%)
    reduce_scatter x3, waiting for transfers between devices, apply_columns(): lax.psum_scatter(lax.dot_general(design_matrix, values, (((0,), (1,)), ((...  216 us
    all_gather x3, blocking collectives, apply_rows(): lax.all_gather(vector_half, 'samp', axis=1, tiled=True)  106 us
    psum x2, blocking collectives, shards(): lax.psum(jnp.sum(direction * hess_dir, axis=1), ('samp', 'feat'))  99.5 us
    psum x2, blocking collectives, precondition(): projected = lax.psum(projected, ('samp', 'feat'))  98 us
    psum x4, blocking collectives, work_lanes(): xin = jax.lax.psum(xin, dev_j)  63.1 us
  transfers between devices with their start and end apart: 3, of which 3 were waited for; matrix products, arithmetic and copies ran while one was open for 0% of the time, Pallas kernels for 0%

profile of v1, /device:TPU:10, one launch (start us, length us, event | category | flops | bytes accessed | tf_op | source)
XLA Modules:
  0.0 635.9 jit_solution(4179257262181225480)
XLA Ops:
  6.5 0.0 copy-start
  6.5 0.0 reduce-scatter.4.cloned.1.call-start
  6.5 0.7 convert_element_type.24
  7.3 0.8 convert_element_type.23
  8.1 33.0 %all_gather.9 = bf16[16,16384]{1,0:T(8,128)(2,1)S(1)} all-gather(bf16[16,1024]{1,0:T(8,128)(2,1)S(1)} %convert_element_type.23), channel_id=1, replica_groups=mesh['samp'=16,'feat'=2] {'samp'}, dimensions={1}, use_global_device_ids=true | all-gather | bytes 557056 | tf_op jit(solution)/shard_map/all_gather | solution.py:17
  41.1 3.4 fusion.22
  44.4 0.0 copy-start.1
  44.5 2.6 psum.77
  47.1 3.8 convolution_bitcast_fusion.2
  51.0 0.0 reduce-scatter.4.cloned.1.call-update
  51.0 0.0 reduce-scatter.6.cloned.1.call-start
  51.0 0.0 copy-done.3
  51.0 0.6 reduce_min.9
  51.6 0.0 copy-done.2
  51.6 0.6 broadcast_add_fusion
  52.3 73.3 %reduce-scatter.4.cloned.1.call-done = f32[1024,16]{0,1:T(8,128)} async-done(((f32[16384,16]{0,1:T(8,128)}), f32[1024,16]{0,1:T(8,128)}) %reduce-scatter.4.cloned.1.call-update) | async-done | bytes 65552 | tf_op jit(solution)/shard_map/reduce_scatter | solution.py:25
  125.6 0.0 copy-done.1
  125.6 0.9 fusion.2
  126.6 0.4 fusion.23
  127.0 50.1 %psum.78 = f32[16,384]{1,0:T(8,128)S(1)} all-reduce(f32[16,384]{1,0:T(8,128)S(1)} %fusion.23), channel_id=1, replica_groups=mesh['samp'=16,'feat'=2] {'samp','feat'}, use_global_device_ids=true, to_apply=%region_3.0 | all-reduce | flops 6144 | bytes 49152 | tf_op jit(solution)/shard_map/psum | solution.py:42
  177.1 0.7 fusion.21
  177.8 32.0 %all_gather.10 = bf16[16,16384]{1,0:T(8,128)(2,1)S(1)} all-gather(bf16[16,1024]{1,0:T(8,128)(2,1)S(1)} %get-tuple-element.7), channel_id=1, replica_groups=mesh['samp'=16,'feat'=2] {'samp'}, dimensions={1}, use_global_device_ids=true | all-gather | bytes 557056 | tf_op jit(solution)/shard_map/all_gather | solution.py:17
  209.8 3.4 fusion.24
  213.1 2.5 psum.81
  215.6 3.8 convolution_bitcast_fusion.1
  219.5 0.0 reduce-scatter.6.cloned.1.call-update
  219.5 0.0 reduce-scatter.8.cloned.1.call-start
  219.5 71.6 %reduce-scatter.6.cloned.1.call-done = f32[1024,16]{0,1:T(8,128)} async-done(((f32[16384,16]{0,1:T(8,128)}), f32[1024,16]{0,1:T(8,128)}) %reduce-scatter.6.cloned.1.call-update) | async-done | bytes 65552 | tf_op jit(solution)/shard_map/reduce_scatter | solution.py:25
  291.1 1.0 multiply_reduce_fusion.1
  292.1 49.7 %psum.82 = f32[16]{0:T(128)S(1)} all-reduce(f32[16]{0:T(128)S(1)} %get-tuple-element.5), channel_id=1, replica_groups=mesh['samp'=16,'feat'=2] {'samp','feat'}, use_global_device_ids=true, to_apply=%region_10.0 | all-reduce | flops 16 | bytes 128 | tf_op jit(solution)/shard_map/psum | solution.py:68
  341.8 29.1 %psum.79 = f32[16]{0:T(128)S(1)} all-reduce(f32[16]{0:T(128)S(1)} %get-tuple-element.6), channel_id=1, replica_groups=mesh['samp'=16,'feat'=2] {'samp'}, use_global_device_ids=true, to_apply=%region_5.0 | all-reduce | flops 16 | bytes 128 | tf_op jit(solution)/shard_map/psum | solution.py:38
  370.9 2.5 psum.80
  373.4 0.9 multiply_subtract_fusion
  374.3 0.4 fusion.25
  374.7 47.9 %psum.83 = f32[16,384]{1,0:T(8,128)S(1)} all-reduce(f32[16,384]{1,0:T(8,128)S(1)} %fusion.25), channel_id=1, replica_groups=mesh['samp'=16,'feat'=2] {'samp','feat'}, use_global_device_ids=true, to_apply=%region_11.0 | all-reduce | flops 6144 | bytes 49152 | tf_op jit(solution)/shard_map/psum | solution.py:42
  422.7 0.8 multiply_reduce_fusion
  423.5 29.1 %psum.84 = f32[16]{0:T(128)S(1)} all-reduce(f32[16]{0:T(128)S(1)} %get-tuple-element.9), channel_id=1, replica_groups=mesh['samp'=16,'feat'=2] {'samp'}, use_global_device_ids=true, to_apply=%region_13.0 | all-reduce | flops 16 | bytes 128 | tf_op jit(solution)/shard_map/psum | solution.py:38
  452.7 2.5 psum.85
  455.1 0.1 fusion.20
  455.2 41.4 %all_gather.11 = bf16[16,16384]{1,0:T(8,128)(2,1)S(1)} all-gather(bf16[16,1024]{1,0:T(8,128)(2,1)S(1)} %fusion.20), channel_id=1, replica_groups=mesh['samp'=16,'feat'=2] {'samp'}, dimensions={1}, use_global_device_ids=true | all-gather | bytes 557056 | tf_op jit(solution)/shard_map/all_gather | solution.py:17
  496.6 3.4 fusion.26
  499.9 2.5 psum.86
  502.4 3.9 convolution_bitcast_fusion
  506.3 0.0 reduce-scatter.8.cloned.1.call-update
  506.3 71.6 %reduce-scatter.8.cloned.1.call-done = f32[1024,16]{0,1:T(8,128)} async-done(((f32[16384,16]{0,1:T(8,128)}), f32[1024,16]{0,1:T(8,128)}) %reduce-scatter.8.cloned.1.call-update) | async-done | bytes 65552 | tf_op jit(solution)/shard_map/reduce_scatter | solution.py:25
  577.9 1.0 fusion.1
  578.9 49.8 %psum.87 = f32[16]{0:T(128)S(1)} all-reduce(f32[16]{0:T(128)S(1)} %fusion.1), channel_id=1, replica_groups=mesh['samp'=16,'feat'=2] {'samp','feat'}, use_global_device_ids=true, to_apply=%region_18.0 | all-reduce | flops 16 | bytes 128 | tf_op jit(solution)/shard_map/psum | solution.py:68
  628.7 0.7 add_add_fusion
  (6 shorter events, 0.0 us)
Async XLA Ops:
  6.5 120.0 %copy-start = (bf16[1024,384]{1,0:T(8,128)(2,1)S(1)}, bf16[1024,384]{1,0:T(8,128)(2,1)}, u32[]{:S(2)}) copy-start(bf16[1024,384]{1,0:T(8,128)(2,1)} %param.10) | copy-start | bytes 2359300
  6.5 119.1 %reduce-scatter.4.cloned.1.call-start = ((), (), s32[]{:S(2)}) async-start(), calls=%async_computation.3 | async-start | bytes 1114112 | tf_op jit(solution)/shard_map/reduce_scatter | solution.py:25
  44.4 6.6 %copy-start.3 = (f32[384]{0:T(512)S(1)}, f32[384]{0:T(512)}, u32[]{:S(2)}) copy-start(f32[384]{0:T(512)} %param.11) | copy-start | bytes 4612
  44.4 7.2 %copy-start.2 = (f32[16]{0:T(128)S(1)}, f32[16]{0:T(128)}, u32[]{:S(2)}) copy-start(f32[16]{0:T(128)} %param.9) | copy-start | bytes 196
  44.4 81.2 %copy-start.1 = (f32[16,1024]{1,0:T(8,128)S(1)}, f32[16,1024]{1,0:T(8,128)}, u32[]{:S(2)}) copy-start(f32[16,1024]{1,0:T(8,128)} %param.8) | copy-start | bytes 196612
  51.0 240.1 %reduce-scatter.6.cloned.1.call-start = ((), (), s32[]{:S(2)}) async-start(), calls=%async_computation.4 | async-start | bytes 1114112 | tf_op jit(solution)/shard_map/reduce_scatter | solution.py:25
  219.5 358.4 %reduce-scatter.8.cloned.1.call-start = ((), (), s32[]{:S(2)}) async-start(), calls=%async_computation.5 | async-start | bytes 1114112 | tf_op jit(solution)/shard_map/reduce_scatter | solution.py:25
Sparse Core Ops, SparseCore 0:
  51.1 74.4 reduce-scatter.3
  219.6 71.4 reduce-scatter.5
  506.4 71.4 reduce-scatter.7
